TPU v7x, 32 devices: a 4x4x1 block of a 4x4x8 slice. The times are simulated.
32 devices in a mesh: pod: 1 (over z), data: 4 (over y), model: 8 (over x, core).
Axes of the slice: x: 4, y: 4, z: 1, core: 2. Of those that a mesh axis runs over, the one named last changes fastest.
The devices are a block of a 4x4x8 slice.
Arguments:
- x_in: bfloat16 [4, 1024, 2048], P(('pod', 'data'), 'model')
- dy_in: bfloat16 [4, 1024, 2048], P(('pod', 'data'), 'model')
- w_q: bfloat16 [2048, 16, 128], P(None, 'model')
- w_k: bfloat16 [1, 2048, 128], replicated
- w_v: bfloat16 [1, 2048, 128], replicated
- w_o: bfloat16 [16, 128, 2048], P('model')
Outputs:
- output 1: bfloat16 [4, 1024, 2048], P(('pod', 'data'), 'model')
- output 2: float32 [2048, 16, 128], P(('pod', 'data'), 'model')
- output 3: float32 [2048, 128], P(('pod', 'model', 'data'))
- output 4: float32 [2048, 128], P(('pod', 'model', 'data'))
- output 5: float32 [16, 128, 2048], P(('pod', 'model'), None, 'data')
All inputs are finite; a program needn't handle non-finite values.
Results may differ from a plain program's by a relative error of at most 0.00940278.
Values are sent between devices in bfloat16 or wider.
A program may use at most 768 MiB of HBM per device.

v0:
```python
import jax
import jax.numpy as jnp
from jax import lax
from jax.sharding import PartitionSpec as P


def subgroup_pairs(step_shift, sub_size, axis_size):
    return [(start_dev + member, start_dev + (member + step_shift) % sub_size)
            for start_dev in range(0, axis_size, sub_size) for member in range(sub_size)]


def subgroup_scatter_sum(grad_parts, sub_size, axis_size):
    my_slot = lax.axis_index('model') % sub_size
    lead_dim, row_count, col_count = grad_parts.shape
    row_blocks = grad_parts.reshape(lead_dim, sub_size, row_count // sub_size, col_count)
    total_sum = lax.dynamic_index_in_dim(row_blocks, my_slot, axis=1, keepdims=False)
    for step_shift in range(1, sub_size):
        outgoing = lax.dynamic_index_in_dim(row_blocks, (my_slot + step_shift) % sub_size, axis=1, keepdims=False)
        total_sum = total_sum + lax.ppermute(outgoing, 'model', subgroup_pairs(step_shift, sub_size, axis_size))
    return total_sum


def solution(mesh):
    model_size = mesh.shape['model']
    tok_spec = P(('pod', 'data'), 'model', None)

    def device_step(x_loc, dy_loc, w_q, w_k, w_v, w_o):
        kv_heads = w_k.shape[0]
        head_dim = w_k.shape[2]
        sub_size = model_size // kv_heads
        score_scale = head_dim ** -0.5
        kv_index = lax.axis_index('model') // sub_size
        x_full = lax.all_gather(x_loc, 'model', axis=1, tiled=True)
        dy_full = lax.all_gather(dy_loc, 'model', axis=1, tiled=True)
        kv_weights = jnp.stack([lax.dynamic_index_in_dim(w_k, kv_index, axis=0, keepdims=False),
                                lax.dynamic_index_in_dim(w_v, kv_index, axis=0, keepdims=False)])
        seq_len = x_full.shape[1]
        causal = lax.broadcasted_iota(jnp.int32, (seq_len, seq_len), 0) >= lax.broadcasted_iota(jnp.int32, (seq_len, seq_len), 1)
        q_loc = jnp.einsum('btd,dhe->bhte', x_full, w_q, preferred_element_type=jnp.float32).astype(jnp.bfloat16)
        kv_loc = jnp.einsum('btd,nde->nbte', x_full, kv_weights, preferred_element_type=jnp.float32).astype(jnp.bfloat16)
        k_loc = kv_loc[0]
        v_loc = kv_loc[1]
        scores = jnp.einsum('bhqe,bke->bhqk', q_loc, k_loc, preferred_element_type=jnp.float32) * score_scale
        attn_prob = jax.nn.softmax(jnp.where(causal, scores, -jnp.inf), axis=-1)
        prob_bf = attn_prob.astype(jnp.bfloat16)
        out_loc = jnp.einsum('bhqk,bke->bhqe', prob_bf, v_loc, preferred_element_type=jnp.float32).astype(jnp.bfloat16)
        dout_loc = jnp.einsum('btd,hed->bhte', dy_full, w_o, preferred_element_type=jnp.float32).astype(jnp.bfloat16)
        grad_prob = jnp.einsum('bhqe,bke->bhqk', dout_loc, v_loc, preferred_element_type=jnp.float32)
        row_delta = jnp.einsum('bhqe,bhqe->bhq', dout_loc, out_loc, preferred_element_type=jnp.float32)
        grad_score = (attn_prob * (grad_prob - row_delta[..., None])).astype(jnp.bfloat16)
        grad_q = (jnp.einsum('bhqk,bke->bhqe', grad_score, k_loc, preferred_element_type=jnp.float32) * score_scale).astype(jnp.bfloat16)
        grad_k = jnp.einsum('bhqk,bhqe->bke', grad_score, q_loc, preferred_element_type=jnp.float32) * score_scale
        grad_v = jnp.einsum('bhqk,bhqe->bke', prob_bf, dout_loc, preferred_element_type=jnp.float32)
        grad_kv = jnp.stack([grad_k, grad_v]).astype(jnp.bfloat16)
        dx_part = (jnp.einsum('bhte,dhe->btd', grad_q, w_q, preferred_element_type=jnp.float32)
                   + jnp.einsum('nbte,nde->btd', grad_kv, kv_weights, preferred_element_type=jnp.float32))
        dwq_part = jnp.einsum('btd,bhte->dhe', x_full, grad_q, preferred_element_type=jnp.float32)
        dwkv_part = jnp.einsum('btd,nbte->nde', x_full, grad_kv, preferred_element_type=jnp.float32)
        dwo_part = jnp.einsum('bhte,btd->hed', out_loc, dy_full, preferred_element_type=jnp.float32)
        dx_loc = lax.psum_scatter(dx_part, 'model', scatter_dimension=1, tiled=True).astype(jnp.bfloat16)
        dwkv_sub = subgroup_scatter_sum(dwkv_part, sub_size, model_size)
        dwkv_loc = lax.psum_scatter(dwkv_sub, 'data', scatter_dimension=1, tiled=True)
        dwq_loc = lax.psum_scatter(dwq_part, 'data', scatter_dimension=0, tiled=True)
        dwo_loc = lax.psum_scatter(dwo_part, 'data', scatter_dimension=2, tiled=True)
        return dx_loc, dwq_loc, dwkv_loc[0], dwkv_loc[1], dwo_loc

    kv_rows = P(('pod', 'model', 'data'), None)
    return jax.shard_map(device_step, mesh=mesh,
                         in_specs=(tok_spec, tok_spec, P(None, 'model', None), P(), P(), P('model', None, None)),
                         out_specs=(tok_spec, P(('pod', 'data'), 'model', None), kv_rows, kv_rows, P(('pod', 'model'), None, 'data')),
                         check_vma=False)
```

profile of v0, /device:TPU:97, one launch (start us, length us, event | category | flops | bytes accessed | tf_op | source)
XLA Modules:
  0.0 280.4 jit_solution(17317256480965033412)
XLA Ops:
  12.9 30.4 %all-gather.5.cloned.1.call-done = bf16[1,1024,2048]{2,1,0:T(8,128)(2,1)} async-done(((bf16[1,128,2048]{2,1,0:T(8,128)(2,1)}), bf16[1,1024,2048]{2,1,0:T(8,128)(2,1)}) %all-gather.5.cloned.1.call-update) | async-done | bytes 4194320 | tf_op jit(solution)/shard_map/all_gather | solution.py:34
  43.3 4.3 %fusion.32 = bf16[2,1024,128]{1,2,0:T(8,128)(2,1)} fusion(bf16[2,128,2048]{2,1,0:T(8,128)(2,1)S(1)} %copy-done, bf16[1,1024,2048]{2,1,0:T(8,128)(2,1)} %all-gather.5.cloned.1.call-done), kind=kOutput, calls=%fused_computation.32 | convolution fusion | flops 1074003968 | bytes 5767168 | tf_op jit(solution)/shard_map/btd,hed->bhte/dot_general | solution.py:47
  48.8 25.3 %all-gather.3.cloned.1.call-done = bf16[1,1024,2048]{2,1,0:T(8,128)(2,1)} async-done(((bf16[1,128,2048]{2,1,0:T(8,128)(2,1)}), bf16[1,1024,2048]{2,1,0:T(8,128)(2,1)}) %all-gather.3.cloned.1.call-update) | async-done | bytes 4194320 | tf_op jit(solution)/shard_map/all_gather | solution.py:33
  74.1 4.4 %fusion.38 = bf16[2,1024,128]{1,2,0:T(8,128)(2,1)} fusion(bf16[1,1024,2048]{2,1,0:T(8,128)(2,1)} %all-gather.3.cloned.1.call-done, bf16[2048,2,128]{2,1,0:T(2,128)(2,1)S(1)} %copy-done.6), kind=kOutput, calls=%fused_computation.34 | convolution fusion | flops 1074003968 | bytes 5767168 | tf_op jit(solution)/shard_map/btd,dhe->bhte/dot_general | solution.py:39
  78.6 2.1 fusion.35
  80.6 7.3 %fusion.63 = (f32[2,1024]{1,0:T(2,128)S(1)}, f32[2,1024,1024]{1,2,0:T(8,128)}) fusion(pred[1024,1024]{0,1:T(8,128)(4,1)S(1)} %copy-done.7, bf16[2,1024,128]{1,2,0:T(8,128)(2,1)} %fusion.38, bf16[2,1,1024,128]{2,3,0,1:T(8,128)(2,1)} %fusion.35), kind=kOutput, calls=%fused_computation.74 | convolution fusion | flops 545260544 | bytes 10231808 | tf_op jit(solution)/shard_map/sub | solution.py:44
  87.9 4.7 %fusion.18 = bf16[2,1024,1024]{1,2,0:T(8,128)(2,1)S(1)} fusion(f32[2,1024,1024]{1,2,0:T(8,128)} %get-tuple-element.21, f32[2,1024]{1,0:T(2,128)S(1)} %get-tuple-element.20), kind=kLoop, calls=%fused_computation.24 | loop fusion | flops 4194304 | bytes 12591104 | tf_op jit(solution)/shard_map/convert_element_type | solution.py:45
  98.9 2.4 copy-done.3
  103.6 2.6 constant_dynamic-slice_fusion.7
  108.2 1.8 copy.31
  118.9 2.6 collective-permute-start.4
  122.8 11.3 %collective-permute-done.2 = f32[2,256,128]{2,1,0:T(8,128)S(1)} collective-permute-done((f32[2,256,128]{2,1,0:T(8,128)}, f32[2,256,128]{2,1,0:T(8,128)S(1)}, u32[]{:S(2)}, u32[]{:S(2)}) %collective-permute-start.2) | collective-permute-done | bytes 262176 | tf_op jit(solution)/shard_map/ppermute | solution.py:19
  135.9 5.6 %collective-permute-done.5 = f32[2,256,128]{2,1,0:T(8,128)} collective-permute-done((f32[2,256,128]{2,1,0:T(8,128)}, f32[2,256,128]{2,1,0:T(8,128)}, u32[]{:S(2)}, u32[]{:S(2)}) %collective-permute-start.5) | collective-permute-done | bytes 262176 | tf_op jit(solution)/shard_map/ppermute | solution.py:19
  142.2 2.0 fusion.56
  144.4 3.7 %fusion.22 = bf16[2,1024,128]{2,1,0:T(8,128)(2,1)S(1)} fusion(bf16[2,1024,1024]{1,2,0:T(8,128)(2,1)} %copy-done.10, bf16[2,1,1024,128]{2,3,0,1:T(8,128)(2,1)} %fusion.35), kind=kOutput, calls=%fused_computation.27 | convolution fusion | flops 537395200 | bytes 4980736 | tf_op jit(solution)/shard_map/bhqk,bke->bhqe/dot_general | solution.py:51
  148.1 2.6 fusion.19
  150.8 2.5 fusion.47
  153.4 4.5 %fusion.1 = f32[1,1024,2048]{2,1,0:T(8,128)} fusion(f32[1024,2048,1]{1,0,2:T(8,128)S(1)} %fusion.47, bf16[1,2048,128]{1,2,0:T(8,128)(2,1)S(1)} %copy.13, bf16[1,2048,128]{1,2,0:T(8,128)(2,1)S(1)} %copy.12, bf16[1,1024,128]{2,1,0:T(8,128)(2,1)S(1)} %fusion.45, bf16[1,1024,128]{2,1,0:T(8,128)(2,1)S(1)} %fusion.44), kind=kOutput, calls=%fused_computation.2 | convolution fusion | flops 1076625408 | bytes 18350080 | tf_op jit(solution)/shard_map/nbte,nde->btd/dot_general | solution.py:56
  158.0 4.8 %fusion.3 = f32[2,128,2048]{2,1,0:T(8,128)} fusion(bf16[2,1024,128]{2,1,0:T(8,128)(2,1)S(1)} %get-tuple-element.23, bf16[1,1024,2048]{2,1,0:T(8,128)(2,1)} %all-gather.5.cloned.1.call-done), kind=kOutput, calls=%fused_computation.7 | convolution fusion | flops 1073741824 | bytes 6815744 | tf_op jit(solution)/shard_map/bhte,btd->hed/dot_general | solution.py:59
  164.4 27.6 %reduce-scatter.7.cloned.1.call-done = f32[512,2,128]{0,2,1:T(8,128)} async-done(((f32[2048,2,128]{0,2,1:T(8,128)}), f32[512,2,128]{0,2,1:T(8,128)}) %reduce-scatter.7.cloned.1.call-update) | async-done | bytes 524304 | tf_op jit(solution)/shard_map/reduce_scatter | solution.py:63
  192.0 2.0 copy.38
  194.1 49.6 %reduce-scatter.5.cloned.1.call-done = f32[1,128,2048]{2,1,0:T(8,128)} async-done(((f32[1,1024,2048]{2,1,0:T(8,128)}), f32[1,128,2048]{2,1,0:T(8,128)}) %reduce-scatter.5.cloned.1.call-update) | async-done | bytes 1048592 | tf_op jit(solution)/shard_map/reduce_scatter | solution.py:60
  243.6 2.1 convert_element_type.64
  245.7 27.8 %reduce-scatter.11.cloned.1.call-done = f32[2,128,512]{2,1,0:T(8,128)} async-done(((f32[2,128,2048]{2,1,0:T(8,128)}), f32[2,128,512]{2,1,0:T(8,128)}) %reduce-scatter.11.cloned.1.call-update) | async-done | bytes 524304 | tf_op jit(solution)/shard_map/reduce_scatter | solution.py:64
  (65 shorter events, 31.7 us)
Async XLA Ops:
  7.2 36.1 %copy-start = (bf16[2,128,2048]{2,1,0:T(8,128)(2,1)S(1)}, bf16[2,128,2048]{2,1,0:T(8,128)(2,1)}, u32[]{:S(2)}) copy-start(bf16[2,128,2048]{2,1,0:T(8,128)(2,1)} %param.11) | copy-start | bytes 3145732
  7.2 36.1 %all-gather.5.cloned.1.call-start = ((), (), s32[]{:S(2)}) async-start(), calls=%async_computation.5 | async-start | bytes 4718592 | tf_op jit(solution)/shard_map/all_gather | solution.py:34
  8.0 66.1 %all-gather.3.cloned.1.call-start = ((), (), s32[]{:S(2)}) async-start(), calls=%async_computation.4 | async-start | bytes 4718592 | tf_op jit(solution)/shard_map/all_gather | solution.py:33
  8.8 154.2 %reduce-scatter.9.cloned.1.call-start = ((), (), s32[]{:S(2)}) async-start(), calls=%async_computation.8 | async-start | bytes 327680 | tf_op jit(solution)/shard_map/reduce_scatter | solution.py:62
  12.9 61.2 %copy-start.6 = (bf16[2048,2,128]{2,1,0:T(2,128)(2,1)S(1)}, bf16[2048,2,128]{2,1,0:T(2,128)(2,1)}, u32[]{:S(2)}) copy-start(bf16[2048,2,128]{2,1,0:T(2,128)(2,1)} %param.8) | copy-start | bytes 3145732
  74.1 4.4 %copy-start.2 = (bf16[1,1024,2048]{2,1,0:T(8,128)(2,1)S(1)}, bf16[1,1024,2048]{2,1,0:T(8,128)(2,1)}, u32[]{:S(2)}) copy-start(bf16[1,1024,2048]{2,1,0:T(8,128)(2,1)} %all-gather.3.cloned.1.call-done) | copy-start | bytes 12582916
  78.6 2.1 copy-start.7
  87.9 4.7 %copy-start.8 = (bf16[2,1024,128]{1,2,0:T(8,128)(2,1)S(1)}, bf16[2,1024,128]{1,2,0:T(8,128)(2,1)}, u32[]{:S(2)}) copy-start(bf16[2,1024,128]{1,2,0:T(8,128)(2,1)} %fusion.32) | copy-start | bytes 1572868
  87.9 6.0 %copy-start.9 = (bf16[2,1,1024,128]{2,3,0,1:T(8,128)(2,1)S(1)}, bf16[2,1,1024,128]{2,3,0,1:T(8,128)(2,1)}, u32[]{:S(2)}) copy-start(bf16[2,1,1024,128]{2,3,0,1:T(8,128)(2,1)} %fusion.35) | copy-start | bytes 1572868
  92.6 3.4 %copy-start.5 = (f32[2,1024,1024]{1,2,0:T(8,128)S(1)}, f32[2,1024,1024]{1,2,0:T(8,128)}, u32[]{:S(2)}) copy-start(f32[2,1024,1024]{1,2,0:T(8,128)} %get-tuple-element.21) | copy-start | bytes 25165828
  97.7 5.0 %copy-start.10 = (bf16[2,1024,1024]{1,2,0:T(8,128)(2,1)}, bf16[2,1024,1024]{1,2,0:T(8,128)(2,1)S(1)}, u32[]{:S(2)}) copy-start(bf16[2,1024,1024]{1,2,0:T(8,128)(2,1)S(1)} %multiply_convert_fusion) | copy-start | bytes 12582916
  97.7 3.7 %copy-start.3 = (bf16[1,1024,2048]{2,1,0:T(8,128)(2,1)S(1)}, bf16[1,1024,2048]{2,1,0:T(8,128)(2,1)}, u32[]{:S(2)}) copy-start(bf16[1,1024,2048]{2,1,0:T(8,128)(2,1)} %all-gather.3.cloned.1.call-done) | copy-start | bytes 12582916
  107.9 13.6 %collective-permute-start = (f32[2,256,128]{2,1,0:T(8,128)}, f32[2,256,128]{2,1,0:T(8,128)}, u32[]{:S(2)}, u32[]{:S(2)}) collective-permute-start(f32[2,256,128]{2,1,0:T(8,128)} %bitcast.150), channel_id=1, source_target_pairs={{0,1},{1,2},{2,3},{3,4},{4,5},{5,6},{6,7},{7,0},{8,9},{9,10},{10,1... | collective-permute-start | bytes 786440 | tf_op jit(solution)/shard_map/ppermute | solution.py:19
  110.0 11.5 %collective-permute-start.1 = (f32[2,256,128]{2,1,0:T(8,128)}, f32[2,256,128]{2,1,0:T(8,128)}, u32[]{:S(2)}, u32[]{:S(2)}) collective-permute-start(f32[2,256,128]{2,1,0:T(8,128)} %bitcast.149), channel_id=1, source_target_pairs={{0,2},{1,3},{2,4},{3,5},{4,6},{5,7},{6,0},{7,1},{8,10},{9,11},{10,... | collective-permute-start | bytes 786440 | tf_op jit(solution)/shard_map/ppermute | solution.py:19
  116.1 18.0 %collective-permute-start.2 = (f32[2,256,128]{2,1,0:T(8,128)}, f32[2,256,128]{2,1,0:T(8,128)S(1)}, u32[]{:S(2)}, u32[]{:S(2)}) collective-permute-start(f32[2,256,128]{2,1,0:T(8,128)} %bitcast.35), channel_id=1, source_target_pairs={{0,3},{1,4},{2,5},{3,6},{4,7},{5,0},{6,1},{7,2},{8,11},{9,12},{10,... | collective-permute-start | bytes 786440 | tf_op jit(solution)/shard_map/ppermute | solution.py:19
  117.3 16.8 %collective-permute-start.3 = (f32[2,256,128]{2,1,0:T(8,128)}, f32[2,256,128]{2,1,0:T(8,128)S(1)}, u32[]{:S(2)}, u32[]{:S(2)}) collective-permute-start(f32[2,256,128]{2,1,0:T(8,128)} %bitcast.36), channel_id=1, source_target_pairs={{0,4},{1,5},{2,6},{3,7},{4,0},{5,1},{6,2},{7,3},{8,12},{9,13},{10,... | collective-permute-start | bytes 786440 | tf_op jit(solution)/shard_map/ppermute | solution.py:19
  118.9 17.0 %collective-permute-start.4 = (f32[2,256,128]{2,1,0:T(8,128)}, f32[2,256,128]{2,1,0:T(8,128)S(1)}, u32[]{:S(2)}, u32[]{:S(2)}) collective-permute-start(f32[2,256,128]{2,1,0:T(8,128)} %bitcast.148), channel_id=1, source_target_pairs={{0,5},{1,6},{2,7},{3,0},{4,1},{5,2},{6,3},{7,4},{8,13},{9,14},{10,... | collective-permute-start | bytes 786440 | tf_op jit(solution)/shard_map/ppermute | solution.py:19
  121.5 19.9 %collective-permute-start.5 = (f32[2,256,128]{2,1,0:T(8,128)}, f32[2,256,128]{2,1,0:T(8,128)}, u32[]{:S(2)}, u32[]{:S(2)}) collective-permute-start(f32[2,256,128]{2,1,0:T(8,128)} %bitcast.147), channel_id=1, source_target_pairs={{0,6},{1,7},{2,0},{3,1},{4,2},{5,3},{6,4},{7,5},{8,14},{9,15},{10,... | collective-permute-start | bytes 786440 | tf_op jit(solution)/shard_map/ppermute | solution.py:19
  121.5 20.7 %collective-permute-start.6 = (f32[2,256,128]{2,1,0:T(8,128)}, f32[2,256,128]{2,1,0:T(8,128)}, u32[]{:S(2)}, u32[]{:S(2)}) collective-permute-start(f32[2,256,128]{2,1,0:T(8,128)} %bitcast.146), channel_id=1, source_target_pairs={{0,7},{1,0},{2,1},{3,2},{4,3},{5,4},{6,5},{7,6},{8,15},{9,8},{10,9... | collective-permute-start | bytes 786440 | tf_op jit(solution)/shard_map/ppermute | solution.py:19
  144.3 47.7 %reduce-scatter.7.cloned.1.call-start = ((), (), s32[]{:S(2)}) async-start(), calls=%async_computation.7 | async-start | bytes 2621440 | tf_op jit(solution)/shard_map/reduce_scatter | solution.py:63
  144.4 3.7 %copy-start.4 = (bf16[1,1024,2048]{2,1,0:T(8,128)(2,1)S(1)}, bf16[1,1024,2048]{2,1,0:T(8,128)(2,1)}, u32[]{:S(2)}) copy-start(bf16[1,1024,2048]{2,1,0:T(8,128)(2,1)} %all-gather.3.cloned.1.call-done) | copy-start | bytes 12582916
  150.8 92.9 %reduce-scatter.5.cloned.1.call-start = ((), (), s32[]{:S(2)}) async-start(), calls=%async_computation.6 | async-start | bytes 9437184 | tf_op jit(solution)/shard_map/reduce_scatter | solution.py:60
  158.0 115.5 %reduce-scatter.11.cloned.1.call-start = ((), (), s32[]{:S(2)}) async-start(), calls=%async_computation.9 | async-start | bytes 2621440 | tf_op jit(solution)/shard_map/reduce_scatter | solution.py:64
  158.0 115.5 %copy-start.1 = (bf16[2,128,2048]{2,1,0:T(8,128)(2,1)S(1)}, bf16[2,128,2048]{2,1,0:T(8,128)(2,1)}, u32[]{:S(2)}) copy-start(bf16[2,128,2048]{2,1,0:T(8,128)(2,1)} %param.11) | copy-start | bytes 3145732
  (1 other events, 1.6 us)
Sparse Core Ops, SparseCore 0:
  9.7 33.5 all-gather.4
  44.9 29.1 all-gather.2
  144.4 16.4 reduce-scatter.8
  163.1 28.9 reduce-scatter.6
  194.2 49.3 reduce-scatter.4
  246.4 27.0 reduce-scatter.10
where the time goes:
time: 281 us; the launch traced here: 280 us
  waiting for transfers between devices  182 us (65%)
  matrix products  43.1 us (15%)
  local copies, waits for them, and re-layouts  22.6 us (8%)
  between operations  14.5 us (5%)
  other arithmetic  10.1 us (4%)
  starting transfers between devices  8.16 us (3%)
    reduce_scatter x1, waiting for transfers between devices, device_step(): lax.psum_scatter(dx_part, 'model', scatter_dimension=1, tiled=True)  49.6 us
    all_gather x1, waiting for transfers between devices, device_step(): dy_full = lax.all_gather(dy_loc, 'model', axis=1, tiled=True)  30.4 us
    reduce_scatter x1, waiting for transfers between devices, device_step(): lax.psum_scatter(dwo_part, 'data', scatter_dimension=2, tiled=True)  27.8 us
    reduce_scatter x1, waiting for transfers between devices, device_step(): lax.psum_scatter(dwq_part, 'data', scatter_dimension=0, tiled=True)  27.6 us
    all_gather x1, waiting for transfers between devices, device_step(): x_full = lax.all_gather(x_loc, 'model', axis=1, tiled=True)  25.3 us
    ppermute x7, waiting for transfers between devices, subgroup_scatter_sum(): lax.ppermute(outgoing, 'model', subgroup_pairs(step_shift, sub_size, axis...  19.4 us
    unnamed x29, local copies, waits for them, and re-layouts  9.75 us
    dynamic_slice x7, local copies, waits for them, and re-layouts, subgroup_scatter_sum(): lax.dynamic_index_in_dim(row_blocks, (my_slot + step_shift) % sub_size, a...  8.74 us
  transfers between devices with their start and end apart: 13, of which 9 were waited for; matrix products, arithmetic and copies ran while one was open for 14% of the time, Pallas kernels for 0%

commit v1 on v0

v1 whole, which is shorter than its diff:
```python
import functools

import jax
import jax.numpy as jnp
from jax import lax
from jax.experimental import pallas as pl
from jax.experimental.pallas import tpu as pltpu
from jax.sharding import PartitionSpec as P

F32 = jnp.float32
BF16 = jnp.bfloat16
NN = (((1,), (0,)), ((), ()))
NT = (((1,), (1,)), ((), ()))
TN = (((0,), (0,)), ((), ()))


def dot(a, b, dims):
    return lax.dot_general(a, b, dims, preferred_element_type=F32)


def body(cfg, x_hbm, dy_hbm, wq_hbm, wo_hbm, wk_hbm, wv_hbm,
         dx_ref, dwq_ref, dwk_ref, dwv_ref, dwo_ref,
         xf, yf, wq, wo, wkv, qf, kv, of, prob, kvb,
         dxp, dxr, xr, kvp, kvr, kr, dwa, yr, wkp, wkr,
         load_sem, ag_s, ag_r, dd_s, dd_r, xr_s, xr_r, kd_s, kd_r, kr_s, kr_r, yr_s, yr_r, wk_s, wk_r):
    tok, width, head_cols, head_dim, chips, rows = cfg
    half = tok // 2
    chunk = 2 * tok
    seq = chips * chunk
    heads = head_cols // head_dim
    wcol = width // rows
    hcol = width // 2
    hrow = head_cols // 2
    scale = head_dim ** -0.5

    me = lax.axis_index('model')
    cx = me // 2
    cc = me % 2
    cp = 1 - cc
    xright = (cx + 1) % chips
    xleft = (cx + chips - 1) % chips
    xfar = (cx + 2) % chips
    my = lax.axis_index('data')
    yup = (my + 1) % rows
    ydn = (my + rows - 1) % rows
    yfar = (my + 2) % rows
    to_r = {'model': xright * 2 + cc}
    to_l = {'model': xleft * 2 + cc}
    to_p = {'model': cx * 2 + cp}
    to_u = {'data': yup}
    to_d = {'data': ydn}
    to_f = {'data': yfar}

    def rcopy(src, dst, ssem, rsem, dev):
        return pltpu.make_async_remote_copy(src_ref=src, dst_ref=dst, send_sem=ssem, recv_sem=rsem,
                                            device_id=dev, device_id_type=pl.DeviceIdType.MESH)

    bufs = (xf, yf, kvb)

    def piece(arr, xc, core, h):
        return bufs[arr].at[pl.ds((xc * 2 + core) * tok + h * half, half), :]

    def ag_copy(arr, idx, xc, core, h, dev):
        p = piece(arr, xc, core, h)
        return rcopy(p, p, ag_s.at[arr, idx], ag_r.at[arr, (xc * 2 + core) * 2 + h], dev)

    def ag_own(arr):
        return [ag_copy(arr, 0, cx, cc, 0, to_r), ag_copy(arr, 2, cx, cc, 1, to_l),
                ag_copy(arr, 4, cx, cc, 0, to_p), ag_copy(arr, 5, cx, cc, 1, to_p),
                ag_copy(arr, 1, cx, cc, 1, to_r), ag_copy(arr, 3, cx, cc, 0, to_l)]

    def ag_relay(arr):
        return [ag_copy(arr, 6, xleft, cc, 0, to_r), ag_copy(arr, 7, xright, cc, 1, to_l)]

    def ag_cross(arr, idx, xc, h):
        return ag_copy(arr, idx, xc, cc, h, to_p)

    def ag_all_sends(arr):
        out = ag_own(arr) + ag_relay(arr)
        for idx, xc, h in ((8, xleft, 0), (9, xleft, 1), (10, xright, 0), (11, xright, 1), (12, xfar, 0), (13, xfar, 1)):
            out.append(ag_cross(arr, idx, xc, h))
        return out

    def ag_wait(arr, xc, core, h):
        p = piece(arr, xc, core, h)
        rcopy(p, p, ag_s.at[arr, 0], ag_r.at[arr, (xc * 2 + core) * 2 + h], to_p).wait_recv()

    def ag_stage1(arr):
        relays = ag_relay(arr)
        ag_wait(arr, xleft, cc, 0)
        relays[0].start()
        ag_wait(arr, xright, cc, 1)
        relays[1].start()
        ag_cross(arr, 8, xleft, 0).start()
        ag_cross(arr, 11, xright, 1).start()

    def ag_stage2(arr):
        ag_wait(arr, xright, cc, 0)
        ag_cross(arr, 10, xright, 0).start()
        ag_wait(arr, xleft, cc, 1)
        ag_cross(arr, 9, xleft, 1).start()

    def ag_stage3(arr):
        ag_wait(arr, xfar, cc, 0)
        ag_cross(arr, 12, xfar, 0).start()
        ag_wait(arr, xfar, cc, 1)
        ag_cross(arr, 13, xfar, 1).start()

    def ag_partner(arr, xc):
        ag_wait(arr, xc, cp, 0)
        ag_wait(arr, xc, cp, 1)

    def dd_copy(xc):
        return rcopy(dxp.at[xc * 2 + cp], dxr.at[xc], dd_s.at[xc], dd_r.at[xc], to_p)

    def dd_add(xc):
        dd_copy(xc).wait_recv()
        blk = xc * 2 + cc
        dxp[blk] = dxp[blk] + dxr[xc]

    def kd_copy(xc):
        return rcopy(kvp.at[xc * 2 + cp], kvr.at[xc], kd_s.at[xc], kd_r.at[xc], to_p)

    def xpart(xc, h, cl):
        return dxp.at[xc * 2 + cc, pl.ds(h * half, half), pl.ds(cl * hcol, hcol)]

    def kpart(xc, h):
        return kvp.at[xc * 2 + cc, pl.ds(h * half, half), :]

    def ring_src(kind, side):
        if kind == 0:
            return (xright, 1) if side == 0 else (xleft, 0)
        if kind == 1:
            return (xfar, 0) if side == 0 else (xfar, 1)
        return (xright, 0) if side == 0 else (xleft, 1)

    def x_copy(side, kind, cl):
        xc, h = ring_src(kind, side)
        return rcopy(xpart(xc, h, cl), xr.at[side, kind, cl], xr_s.at[side, kind, cl], xr_r.at[side, kind, cl],
                     to_r if side == 0 else to_l)

    def k_copy(side, kind):
        xc, h = ring_src(kind, side)
        return rcopy(kpart(xc, h), kr.at[side, kind], kr_s.at[side, kind], kr_r.at[side, kind],
                     to_r if side == 0 else to_l)

    def x_pass(cl):
        for side in range(2):
            x_copy(side, 1, cl).wait_recv()
            xc, h = ring_src(2, side)
            ref = xpart(xc, h, cl)
            ref[...] = ref[...] + xr[side, 1, cl]
            x_copy(side, 2, cl).start()

    def k_pass():
        for side in range(2):
            k_copy(side, 1).wait_recv()
            xc, h = ring_src(2, side)
            ref = kpart(xc, h)
            ref[...] = ref[...] + kr[side, 1]
            k_copy(side, 2).start()

    def wpart(w, blk, h):
        return dwa.at[w, blk, pl.ds(h * hrow, hrow), :]

    def y_src(kind, side):
        if kind == 0:
            return (yup, 1) if side == 0 else (ydn, 0)
        if kind == 1:
            return (yfar, 0) if side == 0 else (yfar, 1)
        return (yup, 0) if side == 0 else (ydn, 1)

    def y_copy(w, side, kind):
        blk, h = y_src(kind, side)
        return rcopy(wpart(w, blk, h), yr.at[w, side, kind], yr_s.at[w, side, kind], yr_r.at[w, side, kind],
                     to_u if side == 0 else to_d)

    def y_first(w):
        for kind in (1, 0):
            for side in range(2):
                y_copy(w, side, kind).start()

    def y_pass(w):
        for side in range(2):
            y_copy(w, side, 1).wait_recv()
            blk, h = y_src(2, side)
            ref = wpart(w, blk, h)
            ref[...] = ref[...] + yr[w, side, 1]
            y_copy(w, side, 2).start()

    def y_final(w):
        for side in range(2):
            y_copy(w, side, 0).wait_recv()
            y_copy(w, side, 2).wait_recv()
        top = dwa[w, my, 0:hrow, :] + yr[w, 1, 0] + yr[w, 0, 2]
        low = dwa[w, my, hrow:, :] + yr[w, 0, 0] + yr[w, 1, 2]
        return top, low

    own_rows = pl.ds(me * tok, tok)
    loads = [pltpu.make_async_copy(x_hbm, xf.at[own_rows, :], load_sem.at[0]),
             pltpu.make_async_copy(dy_hbm, yf.at[own_rows, :], load_sem.at[1]),
             pltpu.make_async_copy(wq_hbm, wq, load_sem.at[2]),
             pltpu.make_async_copy(wk_hbm, wkv.at[:, pl.ds(0, head_dim)], load_sem.at[3]),
             pltpu.make_async_copy(wv_hbm, wkv.at[:, pl.ds(head_dim, head_dim)], load_sem.at[4]),
             pltpu.make_async_copy(wo_hbm, wo, load_sem.at[5])]
    for cp_ in loads:
        cp_.start()
    barrier = pltpu.get_barrier_semaphore()
    for dev in (to_r, to_l, to_p, to_u, to_d, to_f):
        pl.semaphore_signal(barrier, inc=1, device_id=dev, device_id_type=pl.DeviceIdType.MESH)
    pl.semaphore_wait(barrier, 6)
    loads[0].wait()
    for cp_ in ag_own(0):
        cp_.start()
    dwa[...] = jnp.zeros_like(dwa)
    kvp[...] = jnp.zeros_like(kvp)
    for cp_ in loads[1:]:
        cp_.wait()

    def chunk_of(s):
        return (cx + s + s // 2 - 2 * (s // 3)) % chips

    @pl.loop(0, chips)
    def _(s):
        @pl.when(s == 0)
        def _():
            ag_partner(0, cx)

        @pl.when(s == 1)
        def _():
            ag_stage1(0)
            for cp_ in ag_own(1):
                cp_.start()
            ag_stage2(0)
            ag_partner(0, xright)

        @pl.when(s == 2)
        def _():
            ag_partner(0, xleft)

        @pl.when(s == 3)
        def _():
            ag_stage3(0)
            ag_partner(0, xfar)

        r = pl.ds(chunk_of(s) * chunk, chunk)
        xc = xf[r, :]
        qf[r, :] = dot(xc, wq[...], NN).astype(BF16)
        kv[r, :] = dot(xc, wkv[...], NN).astype(BF16)

    @pl.loop(0, chips)
    def _(s):
        @pl.when(s == 2)
        def _():
            ag_stage1(1)

        i = chunk_of(s)
        r = pl.ds(i * chunk, chunk)
        row_id = lax.broadcasted_iota(jnp.int32, (chunk, seq), 0) + i * chunk
        keep = row_id >= lax.broadcasted_iota(jnp.int32, (chunk, seq), 1)
        for h in range(heads):
            hc = pl.ds(h * head_dim, head_dim)
            sc = dot(qf[r, hc], kv[:, 0:head_dim], NT) * scale
            sc = jnp.where(keep, sc, -jnp.inf)
            ex = jnp.exp(sc - jnp.max(sc, axis=-1, keepdims=True))
            pr = ex * (1.0 / jnp.sum(ex, axis=-1, keepdims=True))
            prob[h, r, :] = pr
            of[r, hc] = dot(pr.astype(BF16), kv[:, head_dim:], NN).astype(BF16)

    @pl.loop(0, chips)
    def _(s):
        @pl.when(s == 0)
        def _():
            ag_partner(1, cx)

        @pl.when(s == 1)
        def _():
            ag_stage2(1)
            ag_partner(1, xright)

        @pl.when(s == 2)
        def _():
            ag_partner(1, xleft)

        @pl.when(s == 3)
        def _():
            dd_add(xright)
            x_copy(0, 0, 0).start()
            ag_stage3(1)
            dd_add(xleft)
            x_copy(1, 0, 0).start()
            ag_partner(1, xfar)

        i = chunk_of(s)
        r = pl.ds(i * chunk, chunk)
        yc = yf[r, :]
        oc = of[r, :]
        for j in range(rows):
            dwa[0, j] += dot(oc, yf[r, j * wcol:(j + 1) * wcol], TN)

        @pl.when(s == 3)
        def _():
            y_first(0)

        do = dot(yc, wo[...], NT).astype(BF16)
        od = do.astype(F32) * oc.astype(F32)
        dqs = []
        for h in range(heads):
            hs = slice(h * head_dim, (h + 1) * head_dim)
            dp = dot(do[:, hs], kv[:, head_dim:], NT)
            pr = prob[h, r, :]
            ds = (pr * (dp - jnp.sum(od[:, hs], axis=-1, keepdims=True))).astype(BF16)
            dqs.append((dot(ds, kv[:, 0:head_dim], NN) * scale).astype(BF16))
            dk = dot(ds, qf[r, hs], TN)
            dv = dot(pr.astype(BF16), do[:, hs], TN)
            kvp[:, :, 0:head_dim] += dk.reshape(2 * chips, tok, head_dim)
            kvp[:, :, head_dim:] += dv.reshape(2 * chips, tok, head_dim)
        dq = jnp.concatenate(dqs, axis=1)
        for j in range(rows):
            dwa[1, j] += dot(dq, xf[r, j * wcol:(j + 1) * wcol], TN)
        for j in range(rows):
            dxp[pl.ds(2 * i, 2), :, j * wcol:(j + 1) * wcol] = dot(dq, wq[j * wcol:(j + 1) * wcol, :], NT).reshape(2, tok, wcol)
        dd_copy(i).start()

    kvp[:, :, 0:head_dim] = kvp[:, :, 0:head_dim] * scale
    for xc in range(chips):
        kd_copy(xc).start()
    y_first(1)
    for xc in range(chips):
        kd_copy(xc).wait_recv()
        blk = xc * 2 + cc
        kvp[blk] = kvp[blk] + kvr[xc]
    for kind in (1, 0):
        for side in range(2):
            k_copy(side, kind).start()
    for side in range(2):
        x_copy(side, 0, 1).start()
    dd_add(xfar)
    k_pass()
    for side in range(2):
        x_copy(side, 1, 0).start()
    dd_add(cx)
    y_pass(0)
    for side in range(2):
        k_copy(side, 0).wait_recv()
        k_copy(side, 2).wait_recv()
    own = cx * 2 + cc
    kvb[pl.ds(me * tok, half), :] = (kvp[own, 0:half, :] + kr[1, 0] + kr[0, 2]).astype(BF16)
    kvb[pl.ds(me * tok + half, half), :] = (kvp[own, half:, :] + kr[0, 0] + kr[1, 2]).astype(BF16)
    for cp_ in ag_own(2):
        cp_.start()
    for side in range(2):
        x_copy(side, 1, 1).start()
    ag_stage1(2)
    ag_stage2(2)
    x_pass(0)
    ag_stage3(2)
    ag_partner(2, cx)
    ag_partner(2, xright)
    ag_partner(2, xleft)
    ag_partner(2, xfar)
    mrow = width // (2 * chips)
    krow = mrow // rows
    part = dot(xf[:, pl.ds(pl.multiple_of(me * mrow, mrow), mrow)], kvb[...], TN)
    wkp[...] = part.reshape(rows, krow, head_cols)

    def wk_copy(idx, blk, dev):
        return rcopy(wkp.at[blk], wkr.at[idx], wk_s.at[idx], wk_r.at[idx], dev)

    wk_copies = [wk_copy(0, yup, to_u), wk_copy(1, ydn, to_d), wk_copy(2, yfar, to_f)]
    for cp_ in wk_copies:
        cp_.start()
    x_pass(1)
    y_pass(1)
    top, low = y_final(0)
    dwo_ref[0:hrow, :] = top
    dwo_ref[hrow:, :] = low
    top, low = y_final(1)
    dwq_ref[:, 0:hrow] = top.T
    dwq_ref[:, hrow:] = low.T
    for cp_ in wk_copies:
        cp_.wait_recv()
    wk_sum = wkp[my] + wkr[0] + wkr[1] + wkr[2]
    dwk_ref[...] = wk_sum[:, 0:head_dim]
    dwv_ref[...] = wk_sum[:, head_dim:]
    kv_own = kvb[own_rows, :]
    for cl in range(2):
        cols = slice(cl * hcol, (cl + 1) * hcol)
        kv_term = dot(kv_own, wkv[cols, :], NT)
        for side in range(2):
            x_copy(side, 0, cl).wait_recv()
            x_copy(side, 2, cl).wait_recv()
        dx_ref[0:half, cols] = (kv_term[0:half] + dxp[own, 0:half, cols] + xr[1, 0, cl] + xr[0, 2, cl]).astype(BF16)
        dx_ref[half:, cols] = (kv_term[half:] + dxp[own, half:, cols] + xr[0, 0, cl] + xr[1, 2, cl]).astype(BF16)

    for arr in range(3):
        for cp_ in ag_all_sends(arr):
            cp_.wait_send()
    for xc in range(chips):
        dd_copy(xc).wait_send()
        kd_copy(xc).wait_send()
    for side in range(2):
        for kind in range(3):
            k_copy(side, kind).wait_send()
            for cl in range(2):
                x_copy(side, kind, cl).wait_send()
            for w in range(2):
                y_copy(w, side, kind).wait_send()
    for cp_ in wk_copies:
        cp_.wait_send()


def solution(mesh):
    model_size = mesh.shape['model']
    data_size = mesh.shape['data']
    tok_spec = P(('pod', 'data'), 'model', None)
    chips = model_size // 2

    def device_step(x_loc, dy_loc, w_q, w_k, w_v, w_o):
        tok, width = x_loc.shape[1:]
        head_dim = w_k.shape[2]
        head_cols = w_q.shape[1] * head_dim
        assert chips == 4 and data_size == 4 and w_k.shape[0] == 1 and x_loc.shape[0] == 1
        seq = model_size * tok
        half = tok // 2
        wcol = width // data_size
        krow = width // (model_size * data_size)
        cfg = (tok, width, head_cols, head_dim, chips, data_size)
        vm = pltpu.VMEM
        dma = pltpu.SemaphoreType.DMA
        scratch = [
            vm((seq, width), BF16), vm((seq, width), BF16), vm((width, head_cols), BF16), vm((head_cols, width), BF16),
            vm((width, 2 * head_dim), BF16), vm((seq, head_cols), BF16), vm((seq, 2 * head_dim), BF16), vm((seq, head_cols), BF16),
            vm((head_cols // head_dim, seq, seq), F32), vm((seq, 2 * head_dim), BF16),
            vm((model_size, tok, width), F32), vm((chips, tok, width), F32), vm((2, 3, 2, half, width // 2), F32),
            vm((model_size, tok, 2 * head_dim), F32), vm((chips, tok, 2 * head_dim), F32), vm((2, 3, half, 2 * head_dim), F32),
            vm((2, data_size, head_cols, wcol), F32), vm((2, 2, 3, head_cols // 2, wcol), F32),
            vm((data_size, krow, 2 * head_dim), F32), vm((3, krow, 2 * head_dim), F32),
            dma((6,)), dma((3, 14)), dma((3, 16)), dma((chips,)), dma((chips,)), dma((2, 3, 2)), dma((2, 3, 2)),
            dma((chips,)), dma((chips,)), dma((2, 3)), dma((2, 3)), dma((2, 2, 3)), dma((2, 2, 3)), dma((3,)), dma((3,)),
        ]
        anyspec = pl.BlockSpec(memory_space=pl.ANY)
        vspec = pl.BlockSpec(memory_space=pltpu.VMEM)
        dx, dwq, dwk, dwv, dwo = pl.pallas_call(
            functools.partial(body, cfg),
            out_shape=(jax.ShapeDtypeStruct((tok, width), BF16), jax.ShapeDtypeStruct((wcol, head_cols), F32),
                       jax.ShapeDtypeStruct((krow, head_dim), F32), jax.ShapeDtypeStruct((krow, head_dim), F32),
                       jax.ShapeDtypeStruct((head_cols, wcol), F32)),
            in_specs=[anyspec] * 6,
            out_specs=(vspec,) * 5,
            scratch_shapes=scratch,
            compiler_params=pltpu.CompilerParams(collective_id=0, has_side_effects=True, vmem_limit_bytes=67000000),
            name='attn_bwd',
        )(x_loc[0], dy_loc[0], w_q.reshape(width, head_cols), w_o.reshape(head_cols, width), w_k[0], w_v[0])
        return (dx[None], dwq.reshape(wcol, head_cols // head_dim, head_dim), dwk, dwv,
                dwo.reshape(head_cols // head_dim, head_dim, wcol))

    kv_rows = P(('pod', 'model', 'data'), None)
    return jax.shard_map(device_step, mesh=mesh,
                         in_specs=(tok_spec, tok_spec, P(None, 'model', None), P(), P(), P('model', None, None)),
                         out_specs=(tok_spec, P(('pod', 'data'), 'model', None), kv_rows, kv_rows, P(('pod', 'model'), None, 'data')),
                         check_vma=False)
```

time: 281 us -> 108 us (0.38)
  waiting for transfers between devices: 182 us -> 0 us
  Pallas kernels: 0 us -> 99.5 us
  matrix products: 43.1 us -> 0 us
  local copies, waits for them, and re-layouts: 22.6 us -> 7.46 us
  between operations: 14.5 us -> 0.65 us
  other arithmetic: 10.1 us -> 0 us
  starting transfers between devices: 8.16 us -> 0 us
    reduce_scatter x4 -> x0, waiting for transfers between devices: 105 us -> none  [the longest x1 49.6 us: device_step(): lax.psum_scatter(dx_part, 'model', scatter_dimension=1, tiled=True)]
    pallas_call x0 -> x1, Pallas kernels: none -> 99.5 us  [device_step(): pl.pallas_call(functools.partial(body, cfg), out_shape=(jax.ShapeDtypeStr...]
    all_gather x2 -> x0, waiting for transfers between devices: 55.7 us -> none  [the longest x1 30.4 us: device_step(): dy_full = lax.all_gather(dy_loc, 'model', axis=1, tiled=True)]
    dot_general x13 -> x0, matrix products: 35.9 us -> none  [the longest x1 4.85 us: device_step(): jnp.einsum('bhte,btd->hed', out_loc, dy_full, preferred_element_type=jnp....]
    ppermute x7 -> x0, waiting for transfers between devices: 19.4 us -> none  [subgroup_scatter_sum(): lax.ppermute(outgoing, 'model', subgroup_pairs(step_shift, sub_size, axis...]
    dynamic_slice x9 -> x0, local copies, waits for them, and re-layouts: 11.4 us -> none  [the longest x7 8.74 us: subgroup_scatter_sum(): lax.dynamic_index_in_dim(row_blocks, (my_slot + step_shift) % sub_size, a...]
    ppermute x7 -> x0, starting transfers between devices: 7.78 us -> none  [subgroup_scatter_sum(): lax.ppermute(outgoing, 'model', subgroup_pairs(step_shift, sub_size, axis...]
    sub x1 -> x0, matrix products: 7.26 us -> none  [device_step(): attn_prob = jax.nn.softmax(jnp.where(causal, scores, -jnp.inf), axis=-1)]
  transfers between devices with their start and end apart: 13 -> 0, of which waited for: 9 -> 0; matrix products, arithmetic and copies ran while one was open for 14% -> 0% of each run, Pallas kernels for 0% -> 0%
where the time goes in v1:
time: 108 us
  Pallas kernels  99.5 us (92%)
  local copies, waits for them, and re-layouts  7.46 us (7%)
    pallas_call x1, Pallas kernels, device_step(): pl.pallas_call(functools.partial(body, cfg), out_shape=(jax.ShapeDtypeStr...  99.5 us
    unnamed x13, local copies, waits for them, and re-layouts  5.31 us

profile of v1, /device:TPU:97, one launch (start us, length us, event | category | flops | bytes accessed | tf_op | source)
XLA Modules:
  0.0 107.6 jit_solution(380536859680518273)
XLA Ops:
  0.6 2.3 %copy.13 = bf16[256,8,2,128]{3,1,2,0:T(8,128)(2,1)} copy(bf16[256,8,2,128]{3,2,1,0:T(2,128)(2,1)} %bitcast.12) | data formatting | bytes 2097152
  3.0 99.5 %attn_bwd.1 = (bf16[128,2048]{1,0:T(8,128)(2,1)}, f32[512,256]{1,0:T(8,128)}, f32[64,128]{1,0:T(8,128)}, f32[64,128]{1,0:T(8,128)}, f32[256,512]{1,0:T(8,128)}) custom-call(bf16[128,2048]{1,0:T(8,128)(2,1)} %bitcast.16, bf16[128,2048]{1,0:T(8,128)(2,1)} %bitcast.17, bf16[2048,256]{1,0:T(8,128)(2,1)} %bitcast.11, bf16[256,2048]{1,0:T(8,128)(2,1)} %bitcast.13, ...), custom_call_target="tpu_custom_call" | custom-call | tf_op jit(solution)/shard_map/attn_bwd/pallas_call | solution.py:444
  102.5 0.0 copy-start.1
  102.5 2.2 %reshape.24 = f32[512,2,128]{2,1,0:T(2,128)} reshape(f32[512,256]{1,0:T(8,128)} %get-tuple-element.11) | data formatting | bytes 1048576 | tf_op jit(solution)/shard_map/reshape | solution.py:455
  104.7 0.0 copy-done.1
  104.7 0.0 copy-start.3
  104.7 0.0 copy-start
  104.7 0.8 copy.18
  105.5 0.0 copy-done.3
  105.5 0.0 copy-start.2
  105.5 0.6 copy.19
  106.1 0.2 copy-done.2
  106.2 0.6 copy.20
  106.8 0.0 copy-done
  106.8 0.8 copy.21
Async XLA Ops:
  102.5 2.2 %copy-start.1 = (bf16[128,2048]{1,0:T(8,128)(2,1)S(1)}, bf16[128,2048]{1,0:T(8,128)(2,1)}, u32[]{:S(2)}) copy-start(bf16[128,2048]{1,0:T(8,128)(2,1)} %get-tuple-element.10) | copy-start | bytes 1572868
  104.7 0.8 copy-start.3
  104.7 2.2 %copy-start = (f32[256,512]{1,0:T(8,128)S(1)}, f32[256,512]{1,0:T(8,128)}, u32[]{:S(2)}) copy-start(f32[256,512]{1,0:T(8,128)} %get-tuple-element.14) | copy-start | bytes 1572868
  105.5 0.8 copy-start.2

commit v2 on v1

v2 whole, which is shorter than its diff:
```python
import functools

import jax
import jax.numpy as jnp
from jax import lax
from jax.experimental import pallas as pl
from jax.experimental.pallas import tpu as pltpu
from jax.sharding import PartitionSpec as P

F32 = jnp.float32
BF16 = jnp.bfloat16
NN = (((1,), (0,)), ((), ()))
NT = (((1,), (1,)), ((), ()))
TN = (((0,), (0,)), ((), ()))


def dot(a, b, dims):
    return lax.dot_general(a, b, dims, preferred_element_type=F32)


def body(cfg, x_hbm, dy_hbm, wq_hbm, wo_hbm, wk_hbm, wv_hbm,
         dx_ref, dwq_ref, dwk_ref, dwv_ref, dwo_ref,
         xf, yf, wq, wo, wkv, wq2, wq2f, qf, kv, of, prob, dsf, dqf, dof, kvb,
         dxp, dxr, xr, kvp, kvr, kr, dwa, yr, wkp, wkr,
         load_sem, ag_s, ag_r, dd_s, dd_r, xr_s, xr_r, kd_s, kd_r, kr_s, kr_r, yr_s, yr_r, wk_s, wk_r):
    tok, width, head_cols, head_dim, chips, rows = cfg
    half = tok // 2
    chunk = 2 * tok
    seq = chips * chunk
    heads = head_cols // head_dim
    wcol = width // (2 * rows)
    pieces = 4
    pcol = width // pieces
    hcol = width // 2
    scale = head_dim ** -0.5

    me = lax.axis_index('model')
    cx = me // 2
    cc = me % 2
    cp = 1 - cc
    xright = (cx + 1) % chips
    xleft = (cx + chips - 1) % chips
    xfar = (cx + 2) % chips
    my = lax.axis_index('data')
    yup = (my + 1) % rows
    ydn = (my + rows - 1) % rows
    yfar = (my + 2) % rows
    to_r = {'model': xright * 2 + cc}
    to_l = {'model': xleft * 2 + cc}
    to_p = {'model': cx * 2 + cp}
    to_u = {'data': yup}
    to_d = {'data': ydn}
    to_f = {'data': yfar}

    def rcopy(src, dst, ssem, rsem, dev):
        return pltpu.make_async_remote_copy(src_ref=src, dst_ref=dst, send_sem=ssem, recv_sem=rsem,
                                            device_id=dev, device_id_type=pl.DeviceIdType.MESH)

    def piece(arr, xc, core, h):
        r = pl.ds((xc * 2 + core) * tok + h * half, half)
        if arr == 0:
            return xf.at[r, :]
        if arr == 3:
            return kvb.at[r, :]
        return yf.at[r, pl.ds((arr - 1) * hcol, hcol)]

    def ag_copy(arr, idx, xc, core, h, dev):
        p = piece(arr, xc, core, h)
        return rcopy(p, p, ag_s.at[arr, idx], ag_r.at[arr, (xc * 2 + core) * 2 + h], dev)

    def ag_first(arr):
        return [ag_copy(arr, 0, cx, cc, 0, to_r), ag_copy(arr, 2, cx, cc, 1, to_l),
                ag_copy(arr, 4, cx, cc, 0, to_p), ag_copy(arr, 5, cx, cc, 1, to_p)]

    def ag_second(arr):
        return [ag_copy(arr, 1, cx, cc, 1, to_r), ag_copy(arr, 3, cx, cc, 0, to_l)]

    def ag_own(arr):
        return ag_first(arr) + ag_second(arr)

    def ag_relay(arr):
        return [ag_copy(arr, 6, xleft, cc, 0, to_r), ag_copy(arr, 7, xright, cc, 1, to_l)]

    def ag_cross(arr, idx, xc, h):
        return ag_copy(arr, idx, xc, cc, h, to_p)

    def ag_all_sends(arr):
        out = ag_own(arr) + ag_relay(arr)
        for idx, xc, h in ((8, xleft, 0), (9, xleft, 1), (10, xright, 0), (11, xright, 1), (12, xfar, 0), (13, xfar, 1)):
            out.append(ag_cross(arr, idx, xc, h))
        return out

    def ag_wait(arr, xc, core, h):
        p = piece(arr, xc, core, h)
        rcopy(p, p, ag_s.at[arr, 0], ag_r.at[arr, (xc * 2 + core) * 2 + h], to_p).wait_recv()

    def ag_stage1(arr):
        relays = ag_relay(arr)
        ag_wait(arr, xleft, cc, 0)
        relays[0].start()
        ag_wait(arr, xright, cc, 1)
        relays[1].start()
        ag_cross(arr, 8, xleft, 0).start()
        ag_cross(arr, 11, xright, 1).start()

    def ag_stage2(arr):
        ag_wait(arr, xright, cc, 0)
        ag_cross(arr, 10, xright, 0).start()
        ag_wait(arr, xleft, cc, 1)
        ag_cross(arr, 9, xleft, 1).start()

    def ag_stage3(arr):
        ag_wait(arr, xfar, cc, 0)
        ag_cross(arr, 12, xfar, 0).start()
        ag_wait(arr, xfar, cc, 1)
        ag_cross(arr, 13, xfar, 1).start()

    def ag_partner(arr, xc):
        ag_wait(arr, xc, cp, 0)
        ag_wait(arr, xc, cp, 1)

    def dd_copy(xc):
        return rcopy(dxp.at[xc * 2 + cp], dxr.at[xc], dd_s.at[xc], dd_r.at[xc], to_p)

    def dd_add(xc):
        dd_copy(xc).wait_recv()
        blk = xc * 2 + cc
        dxp[blk] = dxp[blk] + dxr[xc]

    def kd_copy(xc):
        return rcopy(kvp.at[xc * 2 + cp], kvr.at[xc], kd_s.at[xc], kd_r.at[xc], to_p)

    def xpart(xc, h, cl):
        return dxp.at[xc * 2 + cc, pl.ds(h * half, half), pl.ds(cl * pcol, pcol)]

    def kpart(xc, h):
        return kvp.at[xc * 2 + cc, pl.ds(h * half, half), :]

    def ring_src(kind, side):
        if kind == 0:
            return (xright, 1) if side == 0 else (xleft, 0)
        if kind == 1:
            return (xfar, 0) if side == 0 else (xfar, 1)
        return (xright, 0) if side == 0 else (xleft, 1)

    def x_copy(side, kind, cl):
        xc, h = ring_src(kind, side)
        return rcopy(xpart(xc, h, cl), xr.at[side, kind, cl], xr_s.at[side, kind, cl], xr_r.at[side, kind, cl],
                     to_r if side == 0 else to_l)

    def k_copy(side, kind):
        xc, h = ring_src(kind, side)
        return rcopy(kpart(xc, h), kr.at[side, kind], kr_s.at[side, kind], kr_r.at[side, kind],
                     to_r if side == 0 else to_l)

    def x_pass(cl):
        for side in range(2):
            x_copy(side, 1, cl).wait_recv()
            xc, h = ring_src(2, side)
            ref = xpart(xc, h, cl)
            ref[...] = ref[...] + xr[side, 1, cl]
            x_copy(side, 2, cl).start()

    def k_pass():
        for side in range(2):
            k_copy(side, 1).wait_recv()
            xc, h = ring_src(2, side)
            ref = kpart(xc, h)
            ref[...] = ref[...] + kr[side, 1]
            k_copy(side, 2).start()

    order = ((yfar, 0), (yfar, 1), (yup, 1), (ydn, 0), (yup, 0), (ydn, 1), (my, 0), (my, 1))

    def y_blk(w, kind, side):
        pos = {(1, 0): 0, (1, 1): 1, (0, 0): 2, (0, 1): 3, (2, 0): 4, (2, 1): 5, (3, 0): 6, (3, 1): 7}[kind, side]
        if w == 0:
            return pos
        return order[pos][0] * 2 + order[pos][1]

    def y_copy(w, side, kind):
        return rcopy(dwa.at[w, y_blk(w, kind, side)], yr.at[w, side, kind], yr_s.at[w, side, kind], yr_r.at[w, side, kind],
                     to_u if side == 0 else to_d)

    def dw_block(w, kind, side):
        blk = y_blk(w, kind, side)
        if w == 0:
            dwa[0, blk] = dot(of[...], yf[:, blk * wcol:(blk + 1) * wcol], TN)
        else:
            dwa[1, blk] = dot(dqf[...], xf[:, pl.ds(pl.multiple_of(blk * wcol, wcol), wcol)], TN)

    def y_first(w):
        for kind in (1, 0):
            for side in range(2):
                dw_block(w, kind, side)
                y_copy(w, side, kind).start()

    def y_rest(w):
        for kind in (2, 3):
            for side in range(2):
                dw_block(w, kind, side)

    def y_pass(w):
        for side in range(2):
            y_copy(w, side, 1).wait_recv()
            blk = y_blk(w, 2, side)
            dwa[w, blk] = dwa[w, blk] + yr[w, side, 1]
            y_copy(w, side, 2).start()

    def y_final(w):
        for side in range(2):
            y_copy(w, side, 0).wait_recv()
            y_copy(w, side, 2).wait_recv()
        first = dwa[w, y_blk(w, 3, 0)] + yr[w, 1, 0] + yr[w, 0, 2]
        second = dwa[w, y_blk(w, 3, 1)] + yr[w, 0, 0] + yr[w, 1, 2]
        return first, second

    own_rows = pl.ds(me * tok, tok)
    loads = [pltpu.make_async_copy(x_hbm, xf.at[own_rows, :], load_sem.at[0]),
             pltpu.make_async_copy(wq_hbm, wq2, load_sem.at[1]),
             pltpu.make_async_copy(wk_hbm, wkv.at[:, pl.ds(0, head_dim)], load_sem.at[2]),
             pltpu.make_async_copy(wv_hbm, wkv.at[:, pl.ds(head_dim, head_dim)], load_sem.at[3])]
    for pos, (dest, part) in enumerate(order):
        src = pl.ds(pl.multiple_of((dest * 2 + part) * wcol, wcol), wcol)
        dst = pl.ds(pos * wcol, wcol)
        loads.append(pltpu.make_async_copy(dy_hbm.at[:, src], yf.at[own_rows, dst], load_sem.at[4 + pos]))
        loads.append(pltpu.make_async_copy(wo_hbm.at[:, src], wo.at[:, dst], load_sem.at[12 + pos]))
    for cp_ in loads:
        cp_.start()
    barrier = pltpu.get_barrier_semaphore()
    for dev in (to_r, to_l, to_p, to_u, to_d, to_f):
        pl.semaphore_signal(barrier, inc=1, device_id=dev, device_id_type=pl.DeviceIdType.MESH)
    with jax.named_scope('barrier'):
        pl.semaphore_wait(barrier, 6)
    loads[0].wait()
    for cp_ in ag_own(0):
        cp_.start()
    with jax.named_scope('loadw'):
        for cp_ in loads[1:]:
            cp_.wait()
        step = 2 * width // 8

        @pl.loop(0, 8)
        def _(b):
            r2 = pl.ds(pl.multiple_of(b * step, step), step)
            wq2f[r2, :] = wq2[r2, :].astype(F32)
            r1 = pl.ds(pl.multiple_of(b * (step // 2), step // 2), step // 2)
            for h in range(heads):
                wq[r1, h * head_dim:(h + 1) * head_dim] = wq2f[pl.ds(b * step + h, step // 2, stride=heads), :].astype(BF16)

    def chunk_of(s):
        return (cx + s + s // 2 - 2 * (s // 3)) % chips

    @pl.loop(0, chips)
    def _(s):
        @pl.when(s == 0)
        def _():
            ag_partner(0, cx)

        @pl.when(s == 1)
        def _():
            ag_stage1(0)
            for cp_ in ag_own(1):
                cp_.start()
            for cp_ in ag_first(2):
                cp_.start()
            ag_stage2(0)
            ag_partner(0, xright)

        @pl.when(s == 2)
        def _():
            ag_partner(0, xleft)

        @pl.when(s == 3)
        def _():
            ag_stage3(0)
            ag_partner(0, xfar)

        r = pl.ds(chunk_of(s) * chunk, chunk)
        xc = xf[r, :]
        qf[r, :] = dot(xc, wq[...], NN).astype(BF16)
        kv[r, :] = dot(xc, wkv[...], NN).astype(BF16)

    @pl.loop(0, chips)
    def _(s):
        @pl.when(s == 1)
        def _():
            ag_stage1(1)
            for cp_ in ag_second(2):
                cp_.start()

        @pl.when(s == 2)
        def _():
            ag_stage2(1)

        i = chunk_of(s)
        r = pl.ds(i * chunk, chunk)
        row_id = lax.broadcasted_iota(jnp.int32, (chunk, seq), 0) + i * chunk
        keep = row_id >= lax.broadcasted_iota(jnp.int32, (chunk, seq), 1)
        for h in range(heads):
            hc = pl.ds(h * head_dim, head_dim)
            sc = dot(qf[r, hc], kv[:, 0:head_dim], NT) * scale
            sc = jnp.where(keep, sc, -jnp.inf)
            ex = jnp.exp(sc - jnp.max(sc, axis=-1, keepdims=True))
            pr = ex * (1.0 / jnp.sum(ex, axis=-1, keepdims=True))
            prob[h, r, :] = pr
            of[r, hc] = dot(pr.astype(BF16), kv[:, head_dim:], NN).astype(BF16)

    ag_stage1(2)
    ag_partner(1, cx)
    ag_partner(2, cx)

    @pl.loop(0, chips)
    def _(s):
        @pl.when(s == 1)
        def _():
            with jax.named_scope('b1'):
                ag_stage3(1)
                for xc in (xright, xleft, xfar):
                    ag_partner(1, xc)
            with jax.named_scope('b1y'):
                y_first(0)
            with jax.named_scope('b1w'):
                ag_stage2(2)
                ag_partner(2, xright)

        @pl.when(s == 2)
        def _():
            with jax.named_scope('b2'):
                ag_stage3(2)
                ag_partner(2, xleft)

        @pl.when(s == 3)
        def _():
            with jax.named_scope('b3'):
                dd_add(xright)
                for cl in range(2):
                    x_copy(0, 0, cl).start()
                ag_partner(2, xfar)

        with jax.named_scope('b_comp'):
            i = chunk_of(s)
            r = pl.ds(i * chunk, chunk)
            oc = of[r, :]
            do = dot(yf[r, :], wo[...], NT).astype(BF16)
            dof[r, :] = do
            od = do.astype(F32) * oc.astype(F32)
            for h in range(heads):
                hs = slice(h * head_dim, (h + 1) * head_dim)
                dp = dot(do[:, hs], kv[:, head_dim:], NT)
                ds = (prob[h, r, :] * (dp - jnp.sum(od[:, hs], axis=-1, keepdims=True))).astype(BF16)
                dsf[h, r, :] = ds
                dqf[r, hs] = (dot(ds, kv[:, 0:head_dim], NN) * scale).astype(BF16)
            dq = dqf[r, :]
            for j in range(pieces):
                dxp[pl.ds(2 * i, 2), :, j * pcol:(j + 1) * pcol] = dot(dq, wq[j * pcol:(j + 1) * pcol, :], NT).reshape(2, tok, pcol)
        dd_copy(i).start()

    with jax.named_scope('t00_dkv'):
        dd_add(xleft)
        for cl in range(2):
            x_copy(1, 0, cl).start()
        for kc in range(chips):
            ks = slice(kc * chunk, (kc + 1) * chunk)
            qs = slice(kc * chunk, seq)
            dk = jnp.zeros((chunk, head_dim), F32)
            dv = jnp.zeros((chunk, head_dim), F32)
            for h in range(heads):
                hs = slice(h * head_dim, (h + 1) * head_dim)
                dk = dk + dot(dsf[h, qs, ks], qf[qs, hs], TN)
                dv = dv + dot(prob[h, qs, ks].astype(BF16), dof[qs, hs], TN)
            kvp[2 * kc:2 * kc + 2, :, 0:head_dim] = (dk * scale).reshape(2, tok, head_dim)
            kvp[2 * kc:2 * kc + 2, :, head_dim:] = dv.reshape(2, tok, head_dim)
        for xc in range(chips):
            kd_copy(xc).start()

    def x_send(kind, cl):
        for side in range(2):
            x_copy(side, kind, cl).start()

    own = cx * 2 + cc

    def dx_final(cl):
        cols = slice(cl * pcol, (cl + 1) * pcol)
        kv_term = dot(kvb[own_rows, :], wkv[cols, :], NT)
        for side in range(2):
            x_copy(side, 0, cl).wait_recv()
            x_copy(side, 2, cl).wait_recv()
        dx_ref[0:half, cols] = (kv_term[0:half] + dxp[own, 0:half, cols] + xr[1, 0, cl] + xr[0, 2, cl]).astype(BF16)
        dx_ref[half:, cols] = (kv_term[half:] + dxp[own, half:, cols] + xr[0, 0, cl] + xr[1, 2, cl]).astype(BF16)

    with jax.named_scope('t01_ddfar'):
        dd_add(xfar)
        x_send(1, 0)
    with jax.named_scope('t02_y1'):
        y_first(1)
    with jax.named_scope('t03_kd'):
        for xc in range(chips):
            kd_copy(xc).wait_recv()
            blk = xc * 2 + cc
            kvp[blk] = kvp[blk] + kvr[xc]
        for kind in (1, 0):
            for side in range(2):
                k_copy(side, kind).start()
        x_send(0, 2)
    with jax.named_scope('t04_y0'):
        y_rest(0)
        y_pass(0)
    with jax.named_scope('t05_y1r'):
        y_rest(1)
        dd_add(cx)
    with jax.named_scope('t06_kpass'):
        k_pass()
        x_send(1, 1)
    with jax.named_scope('t07_kfin'):
        for side in range(2):
            k_copy(side, 0).wait_recv()
            k_copy(side, 2).wait_recv()
        kvb[pl.ds(me * tok, half), :] = (kvp[own, 0:half, :] + kr[1, 0] + kr[0, 2]).astype(BF16)
        kvb[pl.ds(me * tok + half, half), :] = (kvp[own, half:, :] + kr[0, 0] + kr[1, 2]).astype(BF16)
        for cp_ in ag_own(3):
            cp_.start()
    with jax.named_scope('t08_xp0'):
        x_pass(0)
    with jax.named_scope('t09_ag'):
        ag_stage1(3)
        x_send(1, 2)
        ag_stage2(3)
    with jax.named_scope('t10_xp1'):
        x_pass(1)
        x_send(1, 3)
        x_send(0, 3)
    with jax.named_scope('t11_ag'):
        ag_stage3(3)
        for xc in (cx, xright, xleft, xfar):
            ag_partner(3, xc)
    mrow = width // (2 * chips)
    krow = mrow // rows
    with jax.named_scope('t12_wk'):
        part = dot(xf[:, pl.ds(pl.multiple_of(me * mrow, mrow), mrow)], kvb[...], TN)
        wkp[...] = part.reshape(rows, krow, 2 * head_dim)

    def wk_copy(idx, blk, dev):
        return rcopy(wkp.at[blk], wkr.at[idx], wk_s.at[idx], wk_r.at[idx], dev)

    wk_copies = [wk_copy(0, yup, to_u), wk_copy(1, ydn, to_d), wk_copy(2, yfar, to_f)]
    for cp_ in wk_copies:
        cp_.start()
    with jax.named_scope('t13_y1'):
        y_pass(1)
    with jax.named_scope('t14_xp2'):
        x_pass(2)
    with jax.named_scope('t15_y0f'):
        first, second = y_final(0)
        dwo_ref[:, 0:wcol] = first
        dwo_ref[:, wcol:] = second
        dx_final(0)
    with jax.named_scope('t16_xp3'):
        x_pass(3)
    with jax.named_scope('t17_y1f'):
        for idx, val in enumerate(y_final(1)):
            val = val.T
            for h in range(heads):
                dwq_ref[pl.ds(idx * wcol * heads + h, wcol, stride=heads), :] = val[:, h * head_dim:(h + 1) * head_dim]
        for cp_ in wk_copies:
            cp_.wait_recv()
        wk_sum = wkp[my] + wkr[0] + wkr[1] + wkr[2]
        dwk_ref[...] = wk_sum[:, 0:head_dim]
        dwv_ref[...] = wk_sum[:, head_dim:]
    for cl in range(1, pieces):
        with jax.named_scope('t18_dx%d' % cl):
            dx_final(cl)

    with jax.named_scope('t19_sends'):
        for arr in range(4):
            for cp_ in ag_all_sends(arr):
                cp_.wait_send()
        for xc in range(chips):
            dd_copy(xc).wait_send()
            kd_copy(xc).wait_send()
        for side in range(2):
            for kind in range(3):
                k_copy(side, kind).wait_send()
                for cl in range(pieces):
                    x_copy(side, kind, cl).wait_send()
                for w in range(2):
                    y_copy(w, side, kind).wait_send()
        for cp_ in wk_copies:
            cp_.wait_send()


def copy_out(*refs):
    n = (len(refs) - 1) // 2
    sem = refs[-1]
    copies = [pltpu.make_async_copy(refs[k], refs[n + k], sem.at[k]) for k in range(n)]
    for cp_ in copies:
        cp_.start()
    for cp_ in copies:
        cp_.wait()


VMEM_LIMIT = 64 * 1000 * 1000


def solution(mesh):
    model_size = mesh.shape['model']
    data_size = mesh.shape['data']
    tok_spec = P(('pod', 'data'), 'model', None)
    chips = model_size // 2

    def device_step(x_loc, dy_loc, w_q, w_k, w_v, w_o):
        tok, width = x_loc.shape[1:]
        head_dim = w_k.shape[2]
        head_cols = w_q.shape[1] * head_dim
        assert chips == 4 and data_size == 4 and w_k.shape[0] == 1 and x_loc.shape[0] == 1
        seq = model_size * tok
        half = tok // 2
        heads = head_cols // head_dim
        wcol = width // (2 * data_size)
        krow = width // (model_size * data_size)
        cfg = (tok, width, head_cols, head_dim, chips, data_size)
        vm = pltpu.VMEM
        dma = pltpu.SemaphoreType.DMA
        pieces = 4
        scratch = [
            vm((seq, width), BF16), vm((seq, width), BF16), vm((width, head_cols), BF16), vm((head_cols, width), BF16),
            vm((width, 2 * head_dim), BF16), vm((heads * width, head_dim), BF16), vm((heads * width, head_dim), F32),
            vm((seq, head_cols), BF16), vm((seq, 2 * head_dim), BF16), vm((seq, head_cols), BF16),
            vm((heads, seq, seq), F32), vm((heads, seq, seq), BF16), vm((seq, head_cols), BF16), vm((seq, head_cols), BF16),
            vm((seq, 2 * head_dim), BF16),
            vm((model_size, tok, width), F32), vm((chips, tok, width), F32), vm((2, 3, pieces, half, width // pieces), F32),
            vm((model_size, tok, 2 * head_dim), F32), vm((chips, tok, 2 * head_dim), F32), vm((2, 3, half, 2 * head_dim), F32),
            vm((2, 2 * data_size, head_cols, wcol), F32), vm((2, 2, 3, head_cols, wcol), F32),
            vm((data_size, krow, 2 * head_dim), F32), vm((3, krow, 2 * head_dim), F32),
            dma((20,)), dma((4, 14)), dma((4, 16)), dma((chips,)), dma((chips,)), dma((2, 3, pieces)), dma((2, 3, pieces)),
            dma((chips,)), dma((chips,)), dma((2, 3)), dma((2, 3)), dma((2, 2, 3)), dma((2, 2, 3)), dma((3,)), dma((3,)),
        ]
        anyspec = pl.BlockSpec(memory_space=pl.ANY)
        vspec = pl.BlockSpec(memory_space=pltpu.VMEM)
        shapes = (jax.ShapeDtypeStruct((tok, width), BF16), jax.ShapeDtypeStruct((heads * 2 * wcol, head_dim), F32),
                  jax.ShapeDtypeStruct((krow, head_dim), F32), jax.ShapeDtypeStruct((krow, head_dim), F32),
                  jax.ShapeDtypeStruct((head_cols, 2 * wcol), F32))
        outs = pl.pallas_call(
            functools.partial(body, cfg),
            out_shape=shapes,
            in_specs=[anyspec] * 6,
            out_specs=(vspec,) * 5,
            scratch_shapes=scratch,
            compiler_params=pltpu.CompilerParams(collective_id=0, has_side_effects=True, vmem_limit_bytes=VMEM_LIMIT),
            name='attn_bwd',
        )(x_loc[0], dy_loc[0], w_q.reshape(width * heads, head_dim), w_o.reshape(head_cols, width), w_k[0], w_v[0])
        dx, dwq, dwk, dwv, dwo = pl.pallas_call(
            copy_out,
            out_shape=shapes,
            in_specs=[vspec] * 5,
            out_specs=(anyspec,) * 5,
            scratch_shapes=[dma((5,))],
            compiler_params=pltpu.CompilerParams(vmem_limit_bytes=4 * 1024 * 1024),
            name='copy_out',
        )(*outs)
        return (dx[None], dwq.reshape(2 * wcol, heads, head_dim), dwk, dwv, dwo.reshape(heads, head_dim, 2 * wcol))

    kv_rows = P(('pod', 'model', 'data'), None)
    return jax.shard_map(device_step, mesh=mesh,
                         in_specs=(tok_spec, tok_spec, P(None, 'model', None), P(), P(), P('model', None, None)),
                         out_specs=(tok_spec, P(('pod', 'data'), 'model', None), kv_rows, kv_rows, P(('pod', 'model'), None, 'data')),
                         check_vma=False)
```

time: 108 us -> 103 us (0.954)
  local copies, waits for them, and re-layouts: 7.46 us -> 4.63 us
  Pallas kernels: 99.5 us -> 96.8 us
    pallas_call x1 -> x2, Pallas kernels: 99.5 us -> 96.8 us  [the longest x1 95.6 us: device_step(): pl.pallas_call(functools.partial(body, cfg), out_shape=shapes, in_specs=[...]
    reshape x1 -> x0, local copies, waits for them, and re-layouts: 2.15 us -> none  [device_step(): dwq.reshape(wcol, head_cols // head_dim, head_dim)]
    unnamed x13 -> x10, local copies, waits for them, and re-layouts: 5.31 us -> 4.63 us
where the time goes in v2:
time: 103 us; the launch traced here: 102 us
  Pallas kernels  96.8 us (94%)
  local copies, waits for them, and re-layouts  4.63 us (4%)
    pallas_call x1, Pallas kernels, device_step(): pl.pallas_call(functools.partial(body, cfg), out_shape=shapes, in_specs=[...  95.6 us
    unnamed x10, local copies, waits for them, and re-layouts  4.63 us

profile of v2, /device:TPU:97, one launch (start us, length us, event | category | flops | bytes accessed | tf_op | source)
XLA Modules:
  0.0 102.2 jit_solution(8827592106230128437)
XLA Ops:
  0.6 95.6 %attn_bwd.1 = (bf16[128,2048]{1,0:T(8,128)(2,1)}, f32[1024,128]{1,0:T(8,128)}, f32[64,128]{1,0:T(8,128)}, f32[64,128]{1,0:T(8,128)}, f32[256,512]{1,0:T(8,128)}) custom-call(bf16[128,2048]{1,0:T(8,128)(2,1)} %bitcast.11, bf16[128,2048]{1,0:T(8,128)(2,1)} %bitcast.12, bf16[4096,128]{1,0:T(8,128)(2,1)} %bitcast.9, bf16[256,2048]{1,0:T(8,128)(2,1)} %bitcast.10, ...), custom_call_target="tpu_custom_call" | custom-call | tf_op jit(solution)/shard_map/attn_bwd/pallas_call | solution.py:542
  96.2 0.0 copy-start
  96.2 1.0 %copy-done = bf16[128,2048]{1,0:T(8,128)(2,1)S(1)} copy-done((bf16[128,2048]{1,0:T(8,128)(2,1)S(1)}, bf16[128,2048]{1,0:T(8,128)(2,1)}, u32[]{:S(2)}) %copy-start) | copy-done | bytes 524312
  97.3 0.0 copy-start.1
  97.3 1.0 %copy-done.1 = f32[1024,128]{1,0:T(8,128)S(1)} copy-done((f32[1024,128]{1,0:T(8,128)S(1)}, f32[1024,128]{1,0:T(8,128)}, u32[]{:S(2)}) %copy-start.1) | copy-done | bytes 524312
  98.3 0.0 copy-start.2
  98.3 1.0 %copy-done.2 = f32[256,512]{1,0:T(8,128)S(1)} copy-done((f32[256,512]{1,0:T(8,128)S(1)}, f32[256,512]{1,0:T(8,128)}, u32[]{:S(2)}) %copy-start.2) | copy-done | bytes 524312
  99.3 0.0 copy-start.3
  99.3 0.8 copy-done.3
  100.1 0.0 copy-start.4
  100.1 0.8 copy-done.4
  100.9 1.2 %copy_out.1 = (bf16[128,2048]{1,0:T(8,128)(2,1)}, f32[1024,128]{1,0:T(8,128)}, f32[64,128]{1,0:T(8,128)}, f32[64,128]{1,0:T(8,128)}, f32[256,512]{1,0:T(8,128)}) custom-call(bf16[128,2048]{1,0:T(8,128)(2,1)S(1)} %copy-done, f32[1024,128]{1,0:T(8,128)S(1)} %copy-done.1, f32[64,128]{1,0:T(8,128)S(1)} %copy-done.3, f32[64,128]{1,0:T(8,128)S(1)} %copy-done.4, ...), custom_call_target="tpu_custom_call" | custom-call | tf_op jit(solution)/shard_map/copy_out/pallas_call | solution.py:551
Async XLA Ops:
  96.2 1.0 %copy-start = (bf16[128,2048]{1,0:T(8,128)(2,1)S(1)}, bf16[128,2048]{1,0:T(8,128)(2,1)}, u32[]{:S(2)}) copy-start(bf16[128,2048]{1,0:T(8,128)(2,1)} %get-tuple-element.15.refs_0_) | copy-start | bytes 1572868
  97.3 1.0 %copy-start.1 = (f32[1024,128]{1,0:T(8,128)S(1)}, f32[1024,128]{1,0:T(8,128)}, u32[]{:S(2)}) copy-start(f32[1024,128]{1,0:T(8,128)} %get-tuple-element.16.refs_1_) | copy-start | bytes 1572868
  98.3 1.0 %copy-start.2 = (f32[256,512]{1,0:T(8,128)S(1)}, f32[256,512]{1,0:T(8,128)}, u32[]{:S(2)}) copy-start(f32[256,512]{1,0:T(8,128)} %get-tuple-element.19.refs_4_) | copy-start | bytes 1572868
  99.3 0.8 copy-start.3
  100.1 0.8 copy-start.4
